TPU v7x, 32 devices: a whole 2x2x4 slice. The times are simulated.
32 devices in a mesh: rep: 2 (over x), tp: 4 (over z), sp: 4 (over y, core).
Axes of the slice: x: 2, y: 2, z: 4, core: 2. Of those that a mesh axis runs over, the one named last changes fastest.
Arguments:
- x_in: bfloat16 [1024, 2560], P(('rep', 'sp')), parts along dimension 0
- positions: int32 [1024], P(('rep', 'sp')), parts along dimension 0
- segments: int32 [1024], P(('rep', 'sp')), parts along dimension 0
- gain_attn: float32 [2560], replicated
- w_q: bfloat16 [2560, 4096], P(None, 'tp')
- w_k: bfloat16 [2560, 1024], P(None, 'tp')
- w_v: bfloat16 [2560, 1024], P(None, 'tp')
- w_o: bfloat16 [4096, 2560], P('tp')
- gain_mlp: float32 [2560], replicated
- w_gate: bfloat16 [2560, 9728], P(None, 'tp')
- w_up: bfloat16 [2560, 9728], P(None, 'tp')
- w_down: bfloat16 [9728, 2560], P('tp')
Outputs:
- output 1: bfloat16 [1024, 2560], P(('rep', 'sp')), parts along dimension 0
- output 2: bfloat16 [1024, 16, 128], P('rep', ('tp', 'sp')), parts along dimension 0
- output 3: bfloat16 [1024, 16, 128], P('rep', ('tp', 'sp')), parts along dimension 0
There are 2 independent parts. A program takes and returns all parts, laid end to end along the dimension named above; an argument that names none is the same for every part.
All inputs are finite; a program needn't handle non-finite values.
Results may differ from a plain program's by a relative error of at most 0.0065424.
Values are sent between devices in bfloat16 or wider.
A program may use at most 1 GiB of HBM per device.

v0:
```python
import jax
import jax.numpy as jnp
from jax import lax
from jax.sharding import PartitionSpec as P

HEAD_DIM = 128
ROPE_BASE = 500000.0
NORM_EPS = 1e-5
QUERY_ROWS = 512


def rms_norm(x_f32, gain_vec):
    mean_sq = jnp.mean(x_f32 * x_f32, axis=-1, keepdims=True)
    return (x_f32 * lax.rsqrt(mean_sq + NORM_EPS) * gain_vec).astype(jnp.bfloat16)


def rope_tables(positions):
    half_dim = HEAD_DIM // 2
    inv_freq = jnp.power(jnp.float32(ROPE_BASE), -jnp.arange(half_dim, dtype=jnp.float32) * (2.0 / HEAD_DIM))
    angles = positions.astype(jnp.float32)[..., None] * inv_freq
    return jnp.cos(angles)[..., None, :], jnp.sin(angles)[..., None, :]


def rotate(t_f32, cos_t, sin_t):
    half_dim = HEAD_DIM // 2
    t_lo = t_f32[..., :half_dim]
    t_hi = t_f32[..., half_dim:]
    return jnp.concatenate([t_lo * cos_t - t_hi * sin_t, t_hi * cos_t + t_lo * sin_t], axis=-1)


def project_qkv(x_f32, positions, gain_attn, w_q, w_k, w_v):
    row_count = x_f32.shape[0]
    u_norm = rms_norm(x_f32, gain_attn)
    cos_t, sin_t = rope_tables(positions)
    q_rot = rotate(jnp.dot(u_norm, w_q, preferred_element_type=jnp.float32).reshape(row_count, -1, HEAD_DIM), cos_t, sin_t).astype(jnp.bfloat16)
    k_rot = rotate(jnp.dot(u_norm, w_k, preferred_element_type=jnp.float32).reshape(row_count, -1, HEAD_DIM), cos_t, sin_t).astype(jnp.bfloat16)
    v_proj = jnp.dot(u_norm, w_v, preferred_element_type=jnp.float32).astype(jnp.bfloat16).reshape(row_count, -1, HEAD_DIM)
    return q_rot, k_rot, v_proj


def masked_attention(q_blk, key_rows, val_rows, q_index, k_index, q_seg, k_seg):
    scores = jnp.einsum("qhgc,shc->hgqs", q_blk, key_rows, preferred_element_type=jnp.float32) * (HEAD_DIM ** -0.5)
    allowed = (q_index[:, None] >= k_index[None, :]) & (q_seg[:, None] == k_seg[None, :])
    scores = jnp.where(allowed, scores, -1e30)
    row_max = jnp.max(scores, axis=-1, keepdims=True)
    weights = jnp.exp(scores - row_max)
    prob_bf16 = (weights / jnp.sum(weights, axis=-1, keepdims=True)).astype(jnp.bfloat16)
    return jnp.einsum("hgqs,shc->qhgc", prob_bf16, val_rows, preferred_element_type=jnp.float32).astype(jnp.bfloat16)


def mlp_tail(x_mid, gain_mlp, w_gate, w_up, w_down):
    u_mlp = rms_norm(x_mid, gain_mlp)
    gate_act = jnp.dot(u_mlp, w_gate, preferred_element_type=jnp.float32)
    up_act = jnp.dot(u_mlp, w_up, preferred_element_type=jnp.float32)
    hidden = (jax.nn.silu(gate_act) * up_act).astype(jnp.bfloat16)
    return (x_mid + lax.psum(jnp.dot(hidden, w_down, preferred_element_type=jnp.float32), "tp")).astype(jnp.bfloat16)


def solution(mesh):
    sp_size = mesh.shape["sp"]
    row_spec = P(("rep", "sp"), None)
    tok_spec = P(("rep", "sp"))
    full_spec = P(None)
    col_spec = P(None, "tp")
    wrow_spec = P("tp", None)
    cache_spec = P("rep", ("tp", "sp"), None)

    def local_layer(x_in, positions, segments, gain_attn, w_q, w_k, w_v, w_o, gain_mlp, w_gate, w_up, w_down):
        rows_local = x_in.shape[0]
        tokens = rows_local * sp_size
        heads_local = w_q.shape[1] // HEAD_DIM
        kv_local = w_k.shape[1] // HEAD_DIM
        kv_repeat = max(1, sp_size // kv_local)
        heads_dev = heads_local // sp_size
        slots_dev = kv_local * kv_repeat // sp_size
        group_size = heads_dev // slots_dev
        x_f32 = x_in.astype(jnp.float32)
        q_rot, k_rot, v_proj = project_qkv(x_f32, positions, gain_attn, w_q, w_k, w_v)
        k_send = jnp.repeat(k_rot, kv_repeat, axis=1).reshape(rows_local, sp_size, slots_dev, HEAD_DIM)
        v_send = jnp.repeat(v_proj, kv_repeat, axis=1).reshape(rows_local, sp_size, slots_dev, HEAD_DIM)
        send_buf = jnp.concatenate([q_rot.reshape(rows_local, sp_size, heads_dev, HEAD_DIM), k_send, v_send], axis=2)
        recv_buf = lax.all_to_all(send_buf, "sp", 1, 0, tiled=True).reshape(tokens, heads_dev + 2 * slots_dev, HEAD_DIM)
        seg_all = lax.all_gather(segments, "sp", tiled=True)
        q_all = recv_buf[:, :heads_dev].reshape(tokens, slots_dev, group_size, HEAD_DIM)
        k_all = recv_buf[:, heads_dev:heads_dev + slots_dev]
        v_all = recv_buf[:, heads_dev + slots_dev:]
        tok_index = jnp.arange(tokens)
        block_rows = min(tokens, QUERY_ROWS)
        pieces = []
        for block_idx in range(tokens // block_rows):
            row_start = block_idx * block_rows
            row_stop = row_start + block_rows
            pieces.append(masked_attention(q_all[row_start:row_stop], k_all[:row_stop], v_all[:row_stop],
                                           tok_index[row_start:row_stop], tok_index[:row_stop],
                                           seg_all[row_start:row_stop], seg_all[:row_stop]))
        attn_heads = jnp.concatenate(pieces, axis=0).reshape(sp_size, rows_local, heads_dev, HEAD_DIM)
        attn_local = lax.all_to_all(attn_heads, "sp", 0, 2, tiled=True).reshape(rows_local, heads_local * HEAD_DIM)
        x_mid = x_f32 + lax.psum(jnp.dot(attn_local, w_o, preferred_element_type=jnp.float32), "tp")
        y_out = mlp_tail(x_mid, gain_mlp, w_gate, w_up, w_down)
        return y_out, k_all, v_all

    return jax.shard_map(local_layer, mesh=mesh,
                         in_specs=(row_spec, tok_spec, tok_spec, full_spec, col_spec, col_spec, col_spec, wrow_spec,
                                   full_spec, col_spec, col_spec, wrow_spec),
                         out_specs=(row_spec, cache_spec, cache_spec), check_vma=False)
```

profile of v0, /device:TPU:0, one launch (start us, length us, event | category | flops | bytes accessed | tf_op | source)
XLA Modules:
  0.0 198.9 jit_solution(18274529910674594183)
XLA Ops:
  7.2 0.0 copy-start
  7.2 0.8 convert_element_type.38
  8.0 1.3 fusion.2
  9.3 0.0 copy-start.2
  9.3 0.0 copy-start.7
  9.3 0.0 copy-start.9
  9.3 0.0 copy-done
  9.3 1.6 fusion.6
  10.9 0.0 copy-done.2
  11.0 0.0 copy-done.7
  11.0 0.1 copy-done.9
  11.0 0.4 fusion.16
  11.4 0.1 reshape.130
  11.5 0.3 multiply_cosine_fusion
  11.8 0.3 subtract_convert_fusion.1
  12.1 0.2 pad_maximum_fusion.1
  12.3 3.4 %convolution_bitcast_fusion = f32[16,8,8,128]{3,1,2,0:T(8,128)S(1)} fusion(bf16[2560,1024]{1,0:T(8,128)(2,1)} %param.16, bf16[128,2560]{1,0:T(8,128)(2,1)S(1)} %copy-done.2, f32[2560]{0:T(1024)S(1)} %copy-done.7, f32[128]{0:T(128)S(1)} %add_rsqrt_fusion.1), kind=kOutput, calls=%fused_computation.15 | convolution fusion | flops 672399360 | bytes 6433280 | tf_op jit(solution)/shard_map/dot_general | solution.py:35
  15.7 0.1 copy.40
  15.8 0.3 subtract_convert_fusion
  16.2 0.0 copy-start.8
  16.2 1.0 pad_maximum_fusion
  17.2 4.3 %all-to-all-start = ((bf16[128,4,4,128]{3,0,2,1:T(8,128)(2,1)}), bf16[128,4,4,128]{3,0,2,1:T(8,128)(2,1)S(1)}, u32[]{:S(2)}, u32[]{:S(2)}) async-start(bf16[128,4,4,128]{3,0,2,1:T(8,128)(2,1)} %pad_maximum_fusion), calls=%async_computation | async-start | bytes 1048576 | tf_op jit(solution)/shard_map/all_to_all | solution.py:82
  21.5 0.0 all-reduce.3.cloned.1.call-start
  21.5 0.0 copy-done.8
  21.5 9.4 %all-gather = s32[4,1,128]{2,1,0:T(1,128)S(1)} all-gather(s32[1,1,128]{2,1,0:T(1,128)S(1)} %bitcast.70), channel_id=1, replica_groups=mesh['rep'=2,'tp'=4,'sp'=4] {'sp'}, dimensions={0}, use_global_device_ids=true | all-gather | bytes 2560 | tf_op jit(solution)/shard_map/all_gather | solution.py:83
  30.9 0.2 fusion.8
  31.1 0.0 all-to-all-done
  31.2 0.0 copy-start.5
  31.2 0.0 copy-start.4
  31.2 0.6 fusion.20
  31.8 0.1 copy-done.5
  31.9 0.3 fusion.1
  32.2 0.0 copy-done.4
  32.2 0.5 fusion.5
  32.7 0.1 reshape.136
  32.8 8.4 %all_to_all.30 = bf16[4,128,2,128]{1,3,2,0:T(8,128)(2,1)S(1)} all-to-all(bf16[4,128,2,128]{1,3,2,0:T(8,128)(2,1)S(1)} %copy.35), channel_id=1, replica_groups=mesh['rep'=2,'tp'=4,'sp'=4] {'sp'}, dimensions={0} | all-to-all | bytes 524288 | tf_op jit(solution)/shard_map/all_to_all | solution.py:97
  41.2 4.4 %fusion.21 = f32[128,2560]{1,0:T(8,128)} fusion(bf16[128,1024]{0,1:T(8,128)(2,1)S(1)} %bitcast.65, bf16[1024,2560]{1,0:T(8,128)(2,1)} %param.19), kind=kOutput, calls=%fused_computation.44 | convolution fusion | flops 671088640 | bytes 6815744 | tf_op jit(solution)/shard_map/dot_general | solution.py:98
  45.7 0.0 all-reduce.3.cloned.1.call-update
  45.7 0.0 copy-start.6
  45.7 0.0 all-reduce.5.cloned.1.call-start
  45.7 61.4 %all-reduce.3.cloned.1.call-done = f32[128,2560]{1,0:T(8,128)} async-done(((f32[128,2560]{1,0:T(8,128)}), f32[128,2560]{1,0:T(8,128)}) %all-reduce.3.cloned.1.call-update) | async-done | bytes 1310736 | tf_op jit(solution)/shard_map/psum | solution.py:98
  107.1 0.0 copy-start.3
  107.1 1.7 multiply_reduce_fusion
  108.8 0.0 copy-done.6
  108.8 0.0 copy-done.3
  108.8 0.2 multiply_convert_fusion
  109.1 7.5 %fusion.22 = f32[128,2432]{1,0:T(8,128)} fusion(bf16[128,2560]{1,0:T(8,128)(2,1)S(1)} %multiply_convert_fusion, bf16[2560,2432]{1,0:T(8,128)(2,1)} %param.21), kind=kOutput, calls=%fused_computation.45 | convolution fusion | flops 1593835520 | bytes 14352384 | tf_op jit(solution)/shard_map/dot_general | solution.py:53
  116.5 13.4 %fusion.9 = f32[128,2560]{1,0:T(8,128)} fusion(bf16[2432,2560]{1,0:T(8,128)(2,1)} %param.23, bf16[128,2560]{1,0:T(8,128)(2,1)S(1)} %multiply_convert_fusion, bf16[2560,2432]{1,0:T(8,128)(2,1)} %param.22, f32[128,2432]{1,0:T(8,128)} %fusion.22), kind=kOutput, calls=%fused_computation.23 | convolution fusion | flops 3189538816 | bytes 28114944 | tf_op jit(solution)/shard_map/dot_general | solution.py:56
  129.9 0.0 all-reduce.5.cloned.1.call-update
  129.9 0.0 copy-start.1
  129.9 59.8 %all-reduce.5.cloned.1.call-done = f32[128,2560]{1,0:T(8,128)} async-done(((f32[128,2560]{1,0:T(8,128)}), f32[128,2560]{1,0:T(8,128)}) %all-reduce.5.cloned.1.call-update) | async-done | bytes 1310736 | tf_op jit(solution)/shard_map/psum | solution.py:56
  189.7 2.3 %add_convert_fusion = bf16[128,2560]{1,0:T(8,128)(2,1)} fusion(f32[128,2560]{1,0:T(8,128)} %all-reduce.5.cloned.1.call-done, f32[128,2560]{1,0:T(8,128)S(1)} %copy-done.3, bf16[128,2560]{1,0:T(8,128)(2,1)S(1)} %copy-done.2), kind=kLoop, calls=%fused_computation.12 | loop fusion | flops 1310720 | bytes 3932160 | tf_op jit(solution)/shard_map/convert_element_type | solution.py:56
  192.1 0.0 copy-done.1
  (12 shorter events, 0.3 us)
Async XLA Ops:
  7.2 2.1 %copy-start = (bf16[2560,256]{1,0:T(8,128)(2,1)S(1)}, bf16[2560,256]{1,0:T(8,128)(2,1)}, u32[]{:S(2)}) copy-start(bf16[2560,256]{1,0:T(8,128)(2,1)} %param.18) | copy-start | bytes 3932164
  9.3 1.7 copy-start.2
  9.3 1.7 copy-start.7
  9.3 1.7 copy-start.9
  16.2 5.3 %copy-start.8 = (s32[128]{0:T(128)S(1)}, s32[128]{0:T(128)}, u32[]{:S(2)}) copy-start(s32[128]{0:T(128)} %param.14) | copy-start | bytes 1540
  17.2 14.0 %all-to-all-start = ((bf16[128,4,4,128]{3,0,2,1:T(8,128)(2,1)}), bf16[128,4,4,128]{3,0,2,1:T(8,128)(2,1)S(1)}, u32[]{:S(2)}, u32[]{:S(2)}) async-start(bf16[128,4,4,128]{3,0,2,1:T(8,128)(2,1)} %pad_maximum_fusion), calls=%async_computation | async-start | bytes 1048576 | tf_op jit(solution)/shard_map/all_to_all | solution.py:82
  21.5 85.7 %all-reduce.3.cloned.1.call-start = ((), (), s32[]{:S(2)}) async-start(), calls=%async_computation.2 | async-start | bytes 2621440 | tf_op jit(solution)/shard_map/psum | solution.py:98
  31.2 0.7 copy-start.5
  31.2 1.0 copy-start.4
  45.7 63.1 %copy-start.6 = (f32[2560]{0:T(1024)S(1)}, f32[2560]{0:T(1024)}, u32[]{:S(2)}) copy-start(f32[2560]{0:T(1024)} %param.20) | copy-start | bytes 30724
  45.7 144.0 %all-reduce.5.cloned.1.call-start = ((), (), s32[]{:S(2)}) async-start(), calls=%async_computation.3 | async-start | bytes 2621440 | tf_op jit(solution)/shard_map/psum | solution.py:56
  107.1 1.7 copy-start.3
  129.9 62.2 %copy-start.1 = (bf16[2560,256]{1,0:T(8,128)(2,1)S(1)}, bf16[2560,256]{1,0:T(8,128)(2,1)}, u32[]{:S(2)}) copy-start(bf16[2560,256]{1,0:T(8,128)(2,1)} %param.18) | copy-start | bytes 3932164
Sparse Core Ops, SparseCore 0:
  45.8 61.2 all-reduce.2
  130.0 59.6 all-reduce.4
where the time goes:
time: 199 us
  waiting for transfers between devices  121 us (61%)
  matrix products  31.7 us (16%)
  blocking collectives  17.8 us (9%)
  between operations  14.3 us (7%)
  other arithmetic  8.83 us (4%)
  starting transfers between devices  4.34 us (2%)
    psum x1, waiting for transfers between devices, local_layer(): lax.psum(jnp.dot(attn_local, w_o, preferred_element_type=jnp.float32), 'tp')  61.4 us
    psum x1, waiting for transfers between devices, mlp_tail(): lax.psum(jnp.dot(hidden, w_down, preferred_element_type=jnp.float32), 'tp')  59.8 us
    dot_general x1, matrix products, mlp_tail(): jnp.dot(hidden, w_down, preferred_element_type=jnp.float32)  13.4 us
    all_gather x1, blocking collectives, local_layer(): seg_all = lax.all_gather(segments, 'sp', tiled=True)  9.45 us
    all_to_all x1, blocking collectives, local_layer(): lax.all_to_all(attn_heads, 'sp', 0, 2, tiled=True)  8.39 us
    dot_general x1, matrix products, mlp_tail(): gate_act = jnp.dot(u_mlp, w_gate, preferred_element_type=jnp.float32)  7.47 us
    dot_general x1, matrix products, local_layer(): jnp.dot(attn_local, w_o, preferred_element_type=jnp.float32)  4.43 us
    all_to_all x1, starting transfers between devices, local_layer(): lax.all_to_all(send_buf, 'sp', 1, 0, tiled=True)  4.29 us
  transfers between devices with their start and end apart: 3, of which 2 were waited for; matrix products, arithmetic and copies ran while one was open for 0% of the time, Pallas kernels for 0%

commit v1 on v0

v1 whole, which is shorter than its diff:
```python
import functools

import jax
import jax.numpy as jnp
from jax import lax
from jax.experimental import pallas as pl
from jax.experimental.pallas import tpu as pltpu
from jax.sharding import PartitionSpec as P

HEAD_DIM = 128
ROPE_BASE = 500000.0
NORM_EPS = 1e-5
F32 = jnp.float32
BF16 = jnp.bfloat16
T = 128
D = 2560
QC = 1024
KC = 256
FC = 2432
H = T // 2
PR = 16
PCOLS = D // 2
NR = H // PR
NP1 = 2 * NR
CT = 256
NP2 = D // CT
LAG_FAR = 2
LAG_AGF = 7
LAG_AGN = 9
DIRECT = 2


def norm_rows(x_f32, gain):
    mean_sq = jnp.mean(x_f32 * x_f32, axis=-1, keepdims=True)
    return (x_f32 * lax.rsqrt(mean_sq + NORM_EPS) * gain).astype(BF16)


def dot(a, b):
    return jnp.dot(a, b, preferred_element_type=F32)


def kernel(x_hbm, cs_hbm, segq_hbm, segk_hbm, ga_hbm, wq_hbm, wk_hbm, wv_hbm, wo_hbm, gm_hbm, wg_hbm, wu_hbm, wd_hbm,
           y_hbm, k_hbm, v_hbm,
           x, cs, segq, seg, gains, wq, wk, wv, wo, wg, wu, wd,
           u, q, kv, mask, attn, part1, buf1, xmid, uall, h, part2, buf2, ybuf,
           ld, kv_ss, kv_rs, rl_ss, sg_ss, sg_rs, r1_ss, r1_rs, a1_ss, a1_rs, r2_ss, r2_rs, a2_ss, a2_rs, out_s, c_s):
    me = lax.axis_index("sp")
    z = lax.axis_index("tp")
    pc = me + 1 - 2 * lax.rem(me, 2)
    py = lax.rem(me + 2, 4)
    pd = 3 - me
    lo = z < 2
    is_end = (z == 0) | (z == 3)
    is_mid = (z == 1) | (z == 2)
    dn = jnp.where(lo, 0, 1)
    df = 1 - dn
    rn = pl.multiple_of(jnp.where(lo, H, 0), H)
    rf = pl.multiple_of(jnp.where(lo, 0, H), H)
    z_near = jnp.where(lo, z + 1, z - 1)
    z_far = jnp.where(lo, jnp.maximum(z - 1, 0), jnp.minimum(z + 1, 3))
    mid1 = z_near
    mid2 = jnp.where(lo, 2, 1)
    far_end = jnp.where(lo, 3, 0)

    def load(i, src, dst):
        return pltpu.make_async_copy(src, dst, ld.at[i])

    first = [load(0, x_hbm, x), load(1, ga_hbm, gains.at[0]), load(2, wk_hbm, wk), load(3, cs_hbm, cs),
             load(4, wv_hbm, wv), load(5, segk_hbm, seg.at[me]), load(6, wq_hbm, wq), load(7, segq_hbm, segq)]
    later = [load(8, wo_hbm, wo), load(9, gm_hbm, gains.at[1]), load(10, wg_hbm, wg), load(11, wu_hbm, wu), load(12, wd_hbm, wd)]
    for c in first:
        c.start()

    bar = pltpu.get_barrier_semaphore()
    for s in (pc, py, pd):
        pl.semaphore_signal(bar, inc=1, device_id={"sp": s}, device_id_type=pl.DeviceIdType.MESH)
    for step in (1, 2, 3):
        pl.semaphore_signal(bar, inc=1, device_id={"tp": lax.rem(z + step, 4)}, device_id_type=pl.DeviceIdType.MESH)

    def rcopy(src, dst, ss, rs, **dev):
        return pltpu.make_async_remote_copy(src_ref=src, dst_ref=dst, send_sem=ss, recv_sem=rs, device_id=dev,
                                            device_id_type=pl.DeviceIdType.MESH)

    first[0].wait()
    first[1].wait()
    u[...] = norm_rows(x[...].astype(F32), gains[0])
    first[2].wait()
    first[3].wait()
    cos2 = cs[:, :HEAD_DIM]
    sin2 = cs[:, HEAD_DIM:]

    def rope(t):
        parts = []
        for j in range(t.shape[1] // HEAD_DIM):
            th = t[:, j * HEAD_DIM:(j + 1) * HEAD_DIM]
            parts.append(th * cos2 + pltpu.roll(th, HEAD_DIM // 2, 1) * sin2)
        return jnp.concatenate(parts, axis=1).astype(BF16)

    kv[me, :, 0:KC] = rope(dot(u[...], wk[...]))
    first[4].wait()
    kv[me, :, KC:2 * KC] = dot(u[...], wv[...]).astype(BF16)
    first[5].wait()
    pl.semaphore_wait(bar, 6)
    kv_py = rcopy(kv.at[me], kv.at[me], kv_ss.at[0], kv_rs.at[me], sp=py)
    kv_pc = rcopy(kv.at[me], kv.at[me], kv_ss.at[1], kv_rs.at[me], sp=pc)
    sg = [rcopy(seg.at[me], seg.at[me], sg_ss.at[i], sg_rs.at[me], sp=s) for i, s in enumerate((py, pc, pd))]
    kv_py.start()
    kv_pc.start()
    for c in sg:
        c.start()
    for c in later:
        c.start()
    first[6].wait()

    @pl.loop(0, QC // CT)
    def _(i):
        cols = pl.ds(pl.multiple_of(i * CT, CT), CT)
        q[:, cols] = rope(dot(u[...], wq[:, cols]))

    first[7].wait()

    def kv_in(slot):
        return rcopy(kv.at[slot], kv.at[slot], kv_ss.at[0], kv_rs.at[slot], sp=pc)

    kv_in(py).wait_recv()
    relay = rcopy(kv.at[py], kv.at[py], rl_ss.at[0], kv_rs.at[py], sp=pc)
    relay.start()
    for i, s in enumerate((py, pc, pd)):
        rcopy(seg.at[s], seg.at[s], sg_ss.at[i], sg_rs.at[s], sp=pc).wait_recv()
    q_idx = me * T + lax.broadcasted_iota(jnp.int32, (T, T), 0)
    for b in range(4):
        k_idx = b * T + lax.broadcasted_iota(jnp.int32, (T, T), 1)
        ok = (q_idx >= k_idx) & (segq[...] == seg[b, 0:1, :])
        mask[:, b * T:(b + 1) * T] = jnp.where(ok, 1.0, 0.0)
    kv_in(pc).wait_recv()
    kv_in(pd).wait_recv()

    hsel = me // 2
    caches = []
    for b in range(4):
        for i, dst in enumerate((k_hbm, v_hbm)):
            cols = pl.ds(pl.multiple_of(i * KC + hsel * HEAD_DIM, HEAD_DIM), HEAD_DIM)
            caches.append(pltpu.make_async_copy(kv.at[b, :, cols], dst.at[pl.ds(b * T, T), :], c_s.at[2 * b + i]))
    for c in caches:
        c.start()

    for j in range(8):
        hk = j // 4
        k_h = jnp.concatenate([kv[b, :, hk * HEAD_DIM:(hk + 1) * HEAD_DIM] for b in range(4)], axis=0)
        v_h = jnp.concatenate([kv[b, :, KC + hk * HEAD_DIM:KC + (hk + 1) * HEAD_DIM] for b in range(4)], axis=0)
        sc = lax.dot_general(q[:, j * HEAD_DIM:(j + 1) * HEAD_DIM], k_h, (((1,), (1,)), ((), ())),
                             preferred_element_type=F32) * (HEAD_DIM ** -0.5)
        sc = jnp.where(mask[...] > 0.5, sc, -1e30)
        w = jnp.exp(sc - jnp.max(sc, axis=-1, keepdims=True))
        pr = (w / jnp.sum(w, axis=-1, keepdims=True)).astype(BF16)
        attn[:, j * HEAD_DIM:(j + 1) * HEAD_DIM] = dot(pr, v_h).astype(BF16)

    later[0].wait()

    @pl.loop(0, D // CT)
    def _(i):
        cols = pl.ds(pl.multiple_of(i * CT, CT), CT)
        part1[:, cols] = dot(attn[...], wo[:, cols])

    later[1].wait()

    def piece1(p, base):
        r, c = divmod(p, 2)
        return pl.ds(pl.multiple_of(base + r * PR, PR), PR), pl.ds(c * PCOLS, PCOLS), pl.ds(r * PR, PR)

    def r1_copy(p, d, base, dev):
        rows, cols, brow = piece1(p, base)
        return rcopy(part1.at[rows, cols], buf1.at[d, brow, cols], r1_ss.at[d, p], r1_rs.at[d, p], tp=dev)

    def r1_recv(p, d, base):
        rows, cols, brow = piece1(p, base)
        r1_copy(p, d, base, z_near).wait_recv()
        part1[rows, cols] += buf1[d, brow, cols]

    def ag1_rows(r, base):
        return pl.ds(pl.multiple_of(base + r * PR, PR), PR)

    def ag1_copy(r, d, base, dev, sem):
        rows = ag1_rows(r, base)
        return rcopy(uall.at[rows, :], uall.at[rows, :], a1_ss.at[sem, r], a1_rs.at[d, r], tp=dev)

    @pl.when(is_end)
    def _():
        for p in range(NP1):
            r1_copy(p, dn, rn, z_near).start()
        for r in range(NR):
            for c in range(2):
                r1_copy(2 * r + c, df, rf, z_near).wait_recv()
            rows = ag1_rows(r, rf)
            brow = pl.ds(r * PR, PR)
            xm = x[rows, :].astype(F32) + (part1[rows, :] + buf1[df, brow, :])
            xmid[brow, :] = xm
            uall[rows, :] = norm_rows(xm, gains[1])
            ag1_copy(r, dn, rf, mid1, 0).start()
            if r >= DIRECT:
                ag1_copy(r, dn, rf, mid2, 1).start()
                ag1_copy(r, dn, rf, far_end, 2).start()
        for r in range(NR):
            ag1_copy(r, df, rn, mid1, 0).wait_recv()
        for p in range(NP1):
            r1_copy(p, dn, rn, z_near).wait_send()
        for r in range(NR):
            ag1_copy(r, dn, rf, mid1, 0).wait_send()
            if r >= DIRECT:
                ag1_copy(r, dn, rf, mid2, 1).wait_send()
                ag1_copy(r, dn, rf, far_end, 2).wait_send()

    @pl.when(is_mid)
    def _():
        for s in range(NP1 + LAG_FAR):
            if s < NP1:
                r1_recv(s, dn, rn)
                r1_copy(s, dn, rn, z_near).start()
            if s >= LAG_FAR:
                r1_recv(s - LAG_FAR, df, rf)
                r1_copy(s - LAG_FAR, df, rf, z_far).start()
        for r in range(NR):
            ag1_copy(r, dn, rf, z_near, 0).wait_recv()
            if r < DIRECT:
                ag1_copy(r, dn, rf, z_near, 0).start()
        for r in range(NR):
            ag1_copy(r, df, rn, z_far, 1).wait_recv()
            if r < DIRECT:
                ag1_copy(r, df, rn, z_far, 1).start()
        for p in range(NP1):
            r1_copy(p, dn, rn, z_near).wait_send()
            r1_copy(p, df, rf, z_far).wait_send()
        for r in range(DIRECT):
            ag1_copy(r, dn, rf, z_near, 0).wait_send()
            ag1_copy(r, df, rn, z_far, 1).wait_send()

    later[2].wait()
    later[3].wait()

    def gate_up(cols):
        g = dot(uall[...], wg[:, cols])
        h[:, cols] = (g * jax.nn.sigmoid(g) * dot(uall[...], wu[:, cols])).astype(BF16)

    @pl.loop(0, FC // CT)
    def _(i):
        gate_up(pl.ds(pl.multiple_of(i * CT, CT), CT))

    gate_up(pl.ds((FC // CT) * CT, FC % CT))
    later[4].wait()

    def down(c):
        cols = pl.ds(c * CT, CT)
        part2[:, cols] = dot(h[...], wd[:, cols])

    def r2_copy(c, d, base, dev):
        rows = pl.ds(base, H)
        cols = pl.ds(c * CT, CT)
        return rcopy(part2.at[rows, cols], buf2.at[d, :, cols], r2_ss.at[d, c], r2_rs.at[d, c], tp=dev)

    def r2_recv(c, d, base):
        rows = pl.ds(base, H)
        cols = pl.ds(c * CT, CT)
        r2_copy(c, d, base, z_near).wait_recv()
        part2[rows, cols] += buf2[d, :, cols]

    def ag2_copy(c, d, base, dev, sem):
        rows = pl.ds(base, H)
        cols = pl.ds(c * CT, CT)
        return rcopy(ybuf.at[rows, cols], ybuf.at[rows, cols], a2_ss.at[sem, c], a2_rs.at[d, c], tp=dev)

    def out_copy(c, base, i):
        rows = pl.ds(base, H)
        cols = pl.ds(c * CT, CT)
        return pltpu.make_async_copy(ybuf.at[rows, cols], y_hbm.at[rows, cols], out_s.at[i, c])

    D2 = NP2 - 3

    @pl.when(is_end)
    def _():
        for c in range(NP2):
            down(c)
            r2_copy(c, dn, rn, z_near).start()
        for c in range(NP2):
            r2_copy(c, df, rf, z_near).wait_recv()
            rows = pl.ds(rf, H)
            cols = pl.ds(c * CT, CT)
            ybuf[rows, cols] = (xmid[:, cols] + (part2[rows, cols] + buf2[df, :, cols])).astype(BF16)
            ag2_copy(c, dn, rf, mid1, 0).start()
            if c >= D2:
                ag2_copy(c, dn, rf, mid2, 1).start()
                ag2_copy(c, dn, rf, far_end, 2).start()
            out_copy(c, rf, 0).start()
        for c in range(NP2):
            ag2_copy(c, df, rn, mid1, 0).wait_recv()
            out_copy(c, rn, 1).start()
        for c in range(NP2):
            r2_copy(c, dn, rn, z_near).wait_send()
            ag2_copy(c, dn, rf, mid1, 0).wait_send()
            if c >= D2:
                ag2_copy(c, dn, rf, mid2, 1).wait_send()
                ag2_copy(c, dn, rf, far_end, 2).wait_send()

    @pl.when(is_mid)
    def _():
        for s in range(NP2 + LAG_AGN):
            if s < NP2:
                down(s)
                r2_recv(s, dn, rn)
                r2_copy(s, dn, rn, z_near).start()
            c = s - LAG_FAR
            if 0 <= c < NP2:
                r2_recv(c, df, rf)
                r2_copy(c, df, rf, z_far).start()
            c = s - LAG_AGF
            if 0 <= c < NP2:
                ag2_copy(c, dn, rf, z_near, 0).wait_recv()
                if c < D2:
                    ag2_copy(c, dn, rf, z_near, 0).start()
                out_copy(c, rf, 0).start()
            c = s - LAG_AGN
            if 0 <= c < NP2:
                ag2_copy(c, df, rn, z_far, 1).wait_recv()
                if c < D2:
                    ag2_copy(c, df, rn, z_far, 1).start()
                out_copy(c, rn, 1).start()
        for c in range(NP2):
            r2_copy(c, dn, rn, z_near).wait_send()
            r2_copy(c, df, rf, z_far).wait_send()
            if c < D2:
                ag2_copy(c, dn, rf, z_near, 0).wait_send()
                ag2_copy(c, df, rn, z_far, 1).wait_send()

    for c in range(NP2):
        out_copy(c, rf, 0).wait()
        out_copy(c, rn, 1).wait()
    kv_py.wait_send()
    kv_pc.wait_send()
    relay.wait_send()
    for c in sg:
        c.wait_send()
    for c in caches:
        c.wait()


def rope_tables(positions):
    half_dim = HEAD_DIM // 2
    inv_freq = jnp.power(jnp.float32(ROPE_BASE), -jnp.arange(half_dim, dtype=F32) * (2.0 / HEAD_DIM))
    angles = positions.astype(F32)[:, None] * inv_freq[None, :]
    cos_t, sin_t = jnp.cos(angles), jnp.sin(angles)
    return jnp.concatenate([cos_t, cos_t, -sin_t, sin_t], axis=1)


def local_layer(x_in, positions, segments, gain_attn, w_q, w_k, w_v, w_o, gain_mlp, w_gate, w_up, w_down):
    cs = rope_tables(positions)
    segq = jnp.broadcast_to(segments[:, None], (T, T))
    segk = jnp.broadcast_to(segments[None, :], (8, T))
    dma = pltpu.SemaphoreType.DMA
    vm = pltpu.VMEM
    y, k, v = pl.pallas_call(
        kernel,
        out_shape=[jax.ShapeDtypeStruct((T, D), BF16), jax.ShapeDtypeStruct((4 * T, HEAD_DIM), BF16),
                   jax.ShapeDtypeStruct((4 * T, HEAD_DIM), BF16)],
        in_specs=[pl.BlockSpec(memory_space=pl.ANY)] * 13,
        out_specs=[pl.BlockSpec(memory_space=pl.ANY)] * 3,
        scratch_shapes=[
            vm((T, D), BF16), vm((T, 2 * HEAD_DIM), F32), vm((T, T), jnp.int32), vm((4, 8, T), jnp.int32), vm((2, 1, D), F32),
            vm((D, QC), BF16), vm((D, KC), BF16), vm((D, KC), BF16), vm((QC, D), BF16),
            vm((D, FC), BF16), vm((D, FC), BF16), vm((FC, D), BF16),
            vm((T, D), BF16), vm((T, QC), BF16), vm((4, T, 2 * KC), BF16), vm((T, 4 * T), F32), vm((T, QC), BF16),
            vm((T, D), F32), vm((2, H, D), F32), vm((H, D), F32), vm((T, D), BF16), vm((T, FC), BF16),
            vm((T, D), F32), vm((2, H, D), F32), vm((T, D), BF16),
            dma((13,)), dma((2,)), dma((4,)), dma((1,)), dma((3,)), dma((4,)),
            dma((2, NP1)), dma((2, NP1)), dma((3, NR)), dma((2, NR)),
            dma((2, NP2)), dma((2, NP2)), dma((3, NP2)), dma((2, NP2)), dma((2, NP2)), dma((8,)),
        ],
        compiler_params=pltpu.CompilerParams(collective_id=0, has_side_effects=True, vmem_limit_bytes=67043328),
    )(x_in, cs, segq, segk, gain_attn.reshape(1, D), w_q, w_k, w_v, w_o, gain_mlp.reshape(1, D), w_gate, w_up, w_down)
    return y, k.reshape(4 * T, 1, HEAD_DIM), v.reshape(4 * T, 1, HEAD_DIM)


def solution(mesh):
    row_spec = P(("rep", "sp"), None)
    tok_spec = P(("rep", "sp"))
    col_spec = P(None, "tp")
    wrow_spec = P("tp", None)
    cache_spec = P("rep", ("tp", "sp"), None)
    return jax.shard_map(local_layer, mesh=mesh,
                         in_specs=(row_spec, tok_spec, tok_spec, P(None), col_spec, col_spec, col_spec, wrow_spec,
                                   P(None), col_spec, col_spec, wrow_spec),
                         out_specs=(row_spec, cache_spec, cache_spec), check_vma=False)
```

time: 199 us -> 108 us (0.54)
  waiting for transfers between devices: 121 us -> 0 us
  Pallas kernels: 0 us -> 94.7 us
  matrix products: 31.7 us -> 0 us
  blocking collectives: 17.8 us -> 0 us
  between operations: 14.3 us -> 0.65 us
  local copies, waits for them, and re-layouts: 0.66 us -> 10.3 us
  other arithmetic: 8.83 us -> 1.75 us
  starting transfers between devices: 4.34 us -> 0 us
    psum x2 -> x0, waiting for transfers between devices: 121 us -> none  [the longest x1 61.4 us: local_layer(): lax.psum(jnp.dot(attn_local, w_o, preferred_element_type=jnp.float32), 'tp')]
    pallas_call x0 -> x1, Pallas kernels: none -> 94.7 us  [local_layer(): pl.pallas_call(kernel, out_shape=[jax.ShapeDtypeStruct((T, D), BF16), jax...]
    dot_general x8 -> x0, matrix products: 31.7 us -> none  [the longest x1 13.4 us: mlp_tail(): jnp.dot(hidden, w_down, preferred_element_type=jnp.float32)]
    all_gather x1 -> x0, blocking collectives: 9.45 us -> none  [local_layer(): seg_all = lax.all_gather(segments, 'sp', tiled=True)]
    all_to_all x1 -> x0, blocking collectives: 8.39 us -> none  [local_layer(): lax.all_to_all(attn_heads, 'sp', 0, 2, tiled=True)]
    unnamed x21 -> x3, local copies, waits for them, and re-layouts: 0.3 us -> 5.1 us
    all_to_all x1 -> x0, starting transfers between devices: 4.29 us -> none  [local_layer(): lax.all_to_all(send_buf, 'sp', 1, 0, tiled=True)]
    reduce_sum x3 -> x0, other arithmetic: 3.28 us -> none  [the longest x2 2.97 us: rms_norm(): mean_sq = jnp.mean(x_f32 * x_f32, axis=-1, keepdims=True)]
  transfers between devices with their start and end apart: 3 -> 0, of which waited for: 2 -> 0; matrix products, arithmetic and copies ran while one was open for 0% -> 0% of each run, Pallas kernels for 0% -> 0%
where the time goes in v1:
time: 108 us; the launch traced here: 107 us
  Pallas kernels  94.7 us (88%)
  local copies, waits for them, and re-layouts  10.3 us (10%)
  other arithmetic  1.75 us (2%)
    pallas_call x1, Pallas kernels, local_layer(): pl.pallas_call(kernel, out_shape=[jax.ShapeDtypeStruct((T, D), BF16), jax...  94.7 us
    unnamed x3, local copies, waits for them, and re-layouts  5.1 us

profile of v1, /device:TPU:0, one launch (start us, length us, event | category | flops | bytes accessed | tf_op | source)
XLA Modules:
  0.0 107.4 jit_solution(5543328648042064031)
XLA Ops:
  0.6 0.7 convert_element_type.3
  1.3 1.2 %broadcast_in_dim.5.segk_hbm = s32[8,128]{1,0:T(8,128)} broadcast(s32[128]{0:T(128)} %param.14), dimensions={1} | broadcast | bytes 4608 | tf_op jit(solution)/shard_map/broadcast_in_dim | solution.py:356
  2.5 1.3 %reshape.27.ga_hbm = f32[1,2560]{1,0:T(1,128)} reshape(f32[2560]{0:T(1024)} %param.15) | data formatting | bytes 20480 | tf_op jit(solution)/shard_map/reshape | solution.py:377
  3.9 1.3 %reshape.28.gm_hbm = f32[1,2560]{1,0:T(1,128)} reshape(f32[2560]{0:T(1024)} %param.20) | data formatting | bytes 20480 | tf_op jit(solution)/shard_map/reshape | solution.py:377
  5.2 1.4 %broadcast_in_dim.4.segq_hbm = s32[128,128]{1,0:T(8,128)} broadcast(s32[128]{0:T(128)} %param.14), dimensions={0} | broadcast | bytes 66048 | tf_op jit(solution)/shard_map/broadcast_in_dim | solution.py:355
  6.5 0.3 multiply_cosine_fusion
  6.8 0.8 pad_maximum_fusion.cs_hbm
  7.6 94.7 %shard_map.139 = (bf16[128,2560]{1,0:T(8,128)(2,1)}, bf16[512,128]{1,0:T(8,128)(2,1)}, bf16[512,128]{1,0:T(8,128)(2,1)}) custom-call(bf16[128,2560]{1,0:T(8,128)(2,1)} %x_hbm.1, f32[128,256]{1,0:T(8,128)} %pad_maximum_fusion.cs_hbm, s32[128,128]{1,0:T(8,128)} %broadcast_in_dim.4.segq_hbm, s32[8,128]{1,0:T(8,128)} %broadcast_in_dim.5.segk_hbm, ...), custom_call_target="tpu_custom_call" | custom-call | tf_op jit(solution)/shard_map/pallas_call | solution.py:359
  102.3 2.0 %copy.19 = bf16[128,2560]{1,0:T(8,128)(2,1)} copy(bf16[128,2560]{1,0:T(8,128)(2,1)} %get-tuple-element.15) | data formatting | bytes 1310720
  104.3 1.6 %copy.20 = bf16[512,1,128]{2,0,1:T(8,128)(2,1)} copy(bf16[512,1,128]{2,0,1:T(8,128)(2,1)} %bitcast.3) | data formatting | bytes 262144
  105.8 1.6 %copy.21 = bf16[512,1,128]{2,0,1:T(8,128)(2,1)} copy(bf16[512,1,128]{2,0,1:T(8,128)(2,1)} %bitcast.2) | data formatting | bytes 262144
  (1 shorter events, 0.0 us)

commit v2 on v1

v2 whole, which is shorter than its diff:
```python
import functools

import jax
import jax.numpy as jnp
import numpy as np
from jax import lax
from jax.experimental import pallas as pl
from jax.experimental.pallas import tpu as pltpu
from jax.sharding import PartitionSpec as P

HEAD_DIM = 128
ROPE_BASE = 500000.0
NORM_EPS = 1e-5
F32 = jnp.float32
BF16 = jnp.bfloat16
T = 128
D = 2560
QC = 1024
KC = 256
FC = 2432
H = T // 2
PR = 16
NR = H // PR
NC1 = 4
PC1 = D // NC1
NP1 = NR * NC1
PC2 = 128
NP2 = D // PC2
CT = 256

ROUTE1 = [0, 0, 1, 2]
ROUTE2 = [0] * 16 + [1] * 4
ORDER1 = [
    0, 1, 2, 3, 32, 4, 33, 5, 34, 6, 35, 7, 36, 8, 37, 9, 38, 10, 39, 11, 40, 12, 41, 13, 42, 14, 43, 15, 44, 45, 64,
    46, 47, 65, 96, 98, 66, 97, 99, 67,
]
ORDER2 = [
    0, 1, 2, 3, 4, 32, 5, 33, 6, 34, 7, 35, 8, 36, 9, 37, 10, 38, 11, 39, 12, 40, 13, 41, 14, 42, 15, 43, 16, 44, 17,
    45, 18, 46, 19, 64, 47, 65, 66, 48, 67, 68, 49, 69, 70, 50, 71, 72, 51, 73, 96, 74, 97, 75, 98, 76, 99, 100, 77,
    101, 102, 78, 103, 104, 79, 105, 106, 107, 80, 112, 108, 81, 113, 109, 82, 114, 110, 83, 115, 111,
]


class Reduction:
    def __init__(self, pieces, piece, done, route, order, out, ss, rs, as_, ar):
        self.pieces, self.piece, self.done, self.route, self.order = pieces, piece, done, route, order
        self.out, self.ss, self.rs, self.as_, self.ar = out, ss, rs, as_, ar


def norm_rows(x_f32, gain):
    mean_sq = jnp.mean(x_f32 * x_f32, axis=-1, keepdims=True)
    return (x_f32 * lax.rsqrt(mean_sq + NORM_EPS) * gain).astype(BF16)


def dot(a, b):
    return jnp.dot(a, b, preferred_element_type=F32)


def kernel(x_hbm, pos_hbm, freq_hbm, seg_hbm, ga_hbm, wq_hbm, wk_hbm, wv_hbm, wo_hbm, gm_hbm, wg_hbm, wu_hbm, wd_hbm,
           y_hbm, k_hbm, v_hbm,
           x, pos, freq, seg, segq, cs, ga, gm, wo, wg, wu, wd,
           u, q, kv, mask, attn, part, buf, xmid, uall, h, ybuf,
           ld, kv_ss, kv_rs, rl_ss, sg_ss, sg_rs, r1_ss, r1_rs, a1_ss, a1_rs, r2_ss, r2_rs, a2_ss, a2_rs):
    me = lax.axis_index("sp")
    z = lax.axis_index("tp")
    pc = me + 1 - 2 * lax.rem(me, 2)
    py = lax.rem(me + 2, 4)
    pd = 3 - me
    lo = z < 2
    is_end = (z == 0) | (z == 3)
    is_mid = (z == 1) | (z == 2)
    dn = jnp.where(lo, 0, 1)
    df = 1 - dn
    rn = pl.multiple_of(jnp.where(lo, H, 0), H)
    rf = pl.multiple_of(jnp.where(lo, 0, H), H)
    z_near = jnp.where(lo, z + 1, z - 1)
    z_far = jnp.where(lo, jnp.maximum(z - 1, 0), jnp.minimum(z + 1, 3))
    mid1 = z_near
    mid2 = jnp.where(lo, 2, 1)
    far_end = jnp.where(lo, 3, 0)

    wq, wk, wv = wg.at[:, 0:QC], wg.at[:, QC:QC + KC], wg.at[:, QC + KC:QC + 2 * KC]

    def load(i, src, dst):
        return pltpu.make_async_copy(src, dst, ld.at[i])

    first = [load(0, pos_hbm, pos), load(1, freq_hbm, freq), load(2, seg_hbm, seg.at[me, 0]), load(3, x_hbm, x), load(4, ga_hbm, ga),
             load(5, wk_hbm, wk), load(6, wv_hbm, wv), load(7, wq_hbm, wq)]
    later = [load(8, wo_hbm, wo), load(9, gm_hbm, gm), load(10, wg_hbm, wg), load(11, wu_hbm, wu), load(12, wd_hbm, wd)]
    for c in first:
        c.start()

    bar = pltpu.get_barrier_semaphore()
    for s in (pc, py, pd):
        pl.semaphore_signal(bar, inc=1, device_id={"sp": s}, device_id_type=pl.DeviceIdType.MESH)
    for step in (1, 2, 3):
        pl.semaphore_signal(bar, inc=1, device_id={"tp": lax.rem(z + step, 4)}, device_id_type=pl.DeviceIdType.MESH)

    def rcopy(src, dst, ss, rs, **dev):
        return pltpu.make_async_remote_copy(src_ref=src, dst_ref=dst, send_sem=ss, recv_sem=rs, device_id=dev,
                                            device_id_type=pl.DeviceIdType.MESH)

    first[0].wait()
    first[1].wait()
    lane = lax.broadcasted_iota(jnp.int32, (T, HEAD_DIM), 1)
    angles = jnp.broadcast_to(pos[...].astype(F32).reshape(1, T), (T, T)).T * freq[...]
    cs[:, :HEAD_DIM] = jnp.cos(angles)
    sin_t = jnp.sin(angles)
    cs[:, HEAD_DIM:] = jnp.where(lane < HEAD_DIM // 2, -sin_t, sin_t)
    first[2].wait()
    segq[...] = jnp.broadcast_to(seg[me, 0:1, :].astype(F32), (T, T)).T.astype(jnp.int32)
    first[3].wait()
    first[4].wait()
    u[...] = norm_rows(x[...].astype(F32), ga[...].reshape(1, D))
    first[5].wait()
    cos2 = cs[:, :HEAD_DIM]
    sin2 = cs[:, HEAD_DIM:]

    def rope(t):
        parts = []
        for j in range(t.shape[1] // HEAD_DIM):
            th = t[:, j * HEAD_DIM:(j + 1) * HEAD_DIM]
            parts.append(th * cos2 + pltpu.roll(th, HEAD_DIM // 2, 1) * sin2)
        return jnp.concatenate(parts, axis=1).astype(BF16)

    kv[me, :, 0:KC] = rope(dot(u[...], wk[...]))
    first[6].wait()
    kv[me, :, KC:2 * KC] = dot(u[...], wv[...]).astype(BF16)
    pl.semaphore_wait(bar, 6)
    kv_py = rcopy(kv.at[me], kv.at[me], kv_ss.at[0], kv_rs.at[me], sp=py)
    kv_pc = rcopy(kv.at[me], kv.at[me], kv_ss.at[1], kv_rs.at[me], sp=pc)
    sg = [rcopy(seg.at[me], seg.at[me], sg_ss.at[i], sg_rs.at[me], sp=s) for i, s in enumerate((py, pc, pd))]
    kv_py.start()
    kv_pc.start()
    for c in sg:
        c.start()
    for i in (0, 1, 3, 4):
        later[i].start()
    first[7].wait()

    @pl.loop(0, QC // CT)
    def _(i):
        cols = pl.ds(pl.multiple_of(i * CT, CT), CT)
        qt = dot(u[...], wq[:, cols])
        for j in range(CT // HEAD_DIM):
            q[i * (CT // HEAD_DIM) + j] = rope(qt[:, j * HEAD_DIM:(j + 1) * HEAD_DIM])

    later[2].start()

    def kv_in(slot):
        return rcopy(kv.at[slot], kv.at[slot], kv_ss.at[0], kv_rs.at[slot], sp=pc)

    kv_in(py).wait_recv()
    relay = rcopy(kv.at[py], kv.at[py], rl_ss.at[0], kv_rs.at[py], sp=pc)
    relay.start()
    for i, s in enumerate((py, pc, pd)):
        rcopy(seg.at[s], seg.at[s], sg_ss.at[i], sg_rs.at[s], sp=pc).wait_recv()
    q_idx = me * T + lax.broadcasted_iota(jnp.int32, (T, T), 0)
    for b in range(4):
        k_idx = b * T + lax.broadcasted_iota(jnp.int32, (T, T), 1)
        ok = (q_idx >= k_idx) & (segq[...] == seg[b, 0:1, :])
        mask[:, b * T:(b + 1) * T] = jnp.where(ok, 1.0, 0.0)
    kv_in(pc).wait_recv()
    kv_in(pd).wait_recv()

    hsel = me // 2
    for b in range(4):
        for i, dst in enumerate((k_hbm, v_hbm)):
            cols = pl.ds(pl.multiple_of(i * KC + hsel * HEAD_DIM, HEAD_DIM), HEAD_DIM)
            dst[pl.ds(b * T, T), :] = kv[b, :, cols]

    for hk in range(KC // HEAD_DIM):
        k_h = jnp.concatenate([kv[b, :, hk * HEAD_DIM:(hk + 1) * HEAD_DIM] for b in range(4)], axis=0)
        v_h = jnp.concatenate([kv[b, :, KC + hk * HEAD_DIM:KC + (hk + 1) * HEAD_DIM] for b in range(4)], axis=0)
        sc = lax.dot_general(q[4 * hk:4 * hk + 4].reshape(4 * T, HEAD_DIM), k_h, (((1,), (1,)), ((), ())),
                             preferred_element_type=F32) * (HEAD_DIM ** -0.5)
        sc = jnp.where(mask[...][None] > 0.5, sc.reshape(4, T, 4 * T), -1e30).reshape(4 * T, 4 * T)
        w = jnp.exp(sc - jnp.max(sc, axis=-1, keepdims=True))
        pr = (w * (1.0 / jnp.sum(w, axis=-1, keepdims=True))).astype(BF16)
        ot = dot(pr, v_h).astype(BF16)
        for g in range(4):
            attn[:, (4 * hk + g) * HEAD_DIM:(4 * hk + g + 1) * HEAD_DIM] = ot[g * T:(g + 1) * T]

    later[0].wait()

    @pl.loop(0, D // (2 * CT))
    def _(i):
        cols = pl.ds(pl.multiple_of(i * 2 * CT, CT), 2 * CT)
        part[:, cols] = dot(attn[...], wo[:, cols])

    later[1].wait()

    def r_copy(red, p, d, base, dev):
        rows, cols, brow = red.piece(p, base)
        return rcopy(part.at[rows, cols], buf.at[d, brow, cols], red.ss.at[d, p], red.rs.at[d, p], tp=dev)

    def r_recv(red, p, d, base):
        rows, cols, brow = red.piece(p, base)
        r_copy(red, p, d, base, z_near).wait_recv()
        part[rows, cols] += buf[d, brow, cols]

    def a_copy(red, g, d, base, dev, sem):
        rows, cols = red.done(g, base)
        return rcopy(red.out.at[rows, cols], red.out.at[rows, cols], red.as_.at[sem, g], red.ar.at[d, g], tp=dev)

    def a_targets(red, g):
        return ((mid1,), (mid2, mid1), (far_end, mid2, mid1))[red.route[g]]

    def end_out(red, g):
        for i, dev in enumerate(a_targets(red, g)):
            a_copy(red, g, dn, rf, dev, i).start()

    def end_drain(red):
        for g in range(len(red.route)):
            a_copy(red, g, df, rn, mid1, 0).wait_recv()
        for p in range(red.pieces):
            r_copy(red, p, dn, rn, z_near).wait_send()
        for g in range(len(red.route)):
            for i, dev in enumerate(a_targets(red, g)):
                a_copy(red, g, dn, rf, dev, i).wait_send()

    def mid_all(red):
        for code in red.order:
            kind, p = divmod(code, 32)
            if kind == 0:
                r_recv(red, p, dn, rn)
                r_copy(red, p, dn, rn, z_near).start()
            elif kind == 1:
                r_recv(red, p, df, rf)
                r_copy(red, p, df, rf, z_far).start()
            elif kind == 2:
                a_copy(red, p, dn, rf, z_near, 0).wait_recv()
                if red.route[p] == 0:
                    a_copy(red, p, dn, rf, z_near, 0).start()
            else:
                a_copy(red, p, df, rn, z_far, 1).wait_recv()
                if red.route[p] <= 1:
                    a_copy(red, p, df, rn, z_far, 1).start()
        for p in range(red.pieces):
            r_copy(red, p, dn, rn, z_near).wait_send()
            r_copy(red, p, df, rf, z_far).wait_send()
        for g in range(len(red.route)):
            if red.route[g] == 0:
                a_copy(red, g, dn, rf, z_near, 0).wait_send()
            if red.route[g] <= 1:
                a_copy(red, g, df, rn, z_far, 1).wait_send()

    def row_group(g, base):
        return pl.ds(pl.multiple_of(base + g * PR, PR), PR), pl.ds(0, D)

    def piece1(p, base):
        r, c = divmod(p, NC1)
        return pl.ds(pl.multiple_of(base + r * PR, PR), PR), pl.ds(c * PC1, PC1), pl.ds(r * PR, PR)

    def col_group(g, base):
        return pl.ds(base, H), pl.ds(g * PC2, PC2)

    def piece2(p, base):
        return pl.ds(base, H), pl.ds(p * PC2, PC2), pl.ds(0, H)

    red1 = Reduction(NP1, piece1, row_group, ROUTE1, ORDER1, uall, r1_ss, r1_rs, a1_ss, a1_rs)
    red2 = Reduction(NP2, piece2, col_group, ROUTE2, ORDER2, ybuf, r2_ss, r2_rs, a2_ss, a2_rs)

    @pl.when(is_end)
    def _():
        for p in range(NP1):
            r_copy(red1, p, dn, rn, z_near).start()
        for g in range(NR):
            for c in range(NC1):
                r_copy(red1, NC1 * g + c, df, rf, z_near).wait_recv()
            rows, _ = row_group(g, rf)
            brow = pl.ds(g * PR, PR)
            xm = x[rows, :].astype(F32) + (part[rows, :] + buf[df, brow, :])
            xmid[brow, :] = xm
            uall[rows, :] = norm_rows(xm, gm[...].reshape(1, D))
            end_out(red1, g)
        end_drain(red1)

    @pl.when(is_mid)
    def _():
        mid_all(red1)

    later[2].wait()
    later[3].wait()

    def gate_up(cols):
        g = dot(uall[...], wg[:, cols])
        h[:, cols] = (g * jax.nn.sigmoid(g) * dot(uall[...], wu[:, cols])).astype(BF16)

    @pl.loop(0, FC // CT)
    def _(i):
        gate_up(pl.ds(pl.multiple_of(i * CT, CT), CT))

    gate_up(pl.ds((FC // CT) * CT, FC % CT))
    later[4].wait()

    tiles = [(0, CT), (CT, CT)] + [(c, 2 * CT) for c in range(2 * CT, D, 2 * CT)]

    def down(c, width):
        cols = pl.ds(c, width)
        part[:, cols] = dot(h[...], wd[:, cols])

    @pl.when(is_end)
    def _():
        for c, width in tiles:
            down(c, width)
            for p in range(c // PC2, (c + width) // PC2):
                r_copy(red2, p, dn, rn, z_near).start()
        for p in range(NP2):
            r_copy(red2, p, df, rf, z_near).wait_recv()
            rows, cols = col_group(p, rf)
            ybuf[rows, cols] = (xmid[:, cols] + (part[rows, cols] + buf[df, :, cols])).astype(BF16)
            end_out(red2, p)
        end_drain(red2)

    @pl.when(is_mid)
    def _():
        for c, width in tiles:
            down(c, width)
        mid_all(red2)

    y_hbm[...] = ybuf[...]
    kv_py.wait_send()
    kv_pc.wait_send()
    relay.wait_send()
    for c in sg:
        c.wait_send()


def local_layer(x_in, positions, segments, gain_attn, w_q, w_k, w_v, w_o, gain_mlp, w_gate, w_up, w_down):
    half_dim = HEAD_DIM // 2
    inv_freq = (ROPE_BASE ** (-np.arange(half_dim) * (2.0 / HEAD_DIM))).astype(np.float32)
    freq = jnp.asarray(np.concatenate([inv_freq, inv_freq]).reshape(1, HEAD_DIM))
    operands = (x_in, positions, freq, segments, gain_attn, w_q, w_k, w_v, w_o, gain_mlp, w_gate, w_up, w_down)
    dma = pltpu.SemaphoreType.DMA
    vm = pltpu.VMEM
    y, k, v = pl.pallas_call(
        kernel,
        out_shape=[jax.ShapeDtypeStruct((T, D), BF16), jax.ShapeDtypeStruct((4 * T, HEAD_DIM), BF16),
                   jax.ShapeDtypeStruct((4 * T, HEAD_DIM), BF16)],
        in_specs=[pl.BlockSpec(memory_space=pltpu.HBM)] * 13,
        out_specs=[pl.BlockSpec(memory_space=pltpu.VMEM)] * 3,
        scratch_shapes=[
            vm((T, D), BF16), vm((T,), jnp.int32), vm((1, HEAD_DIM), F32), vm((4, 8, T), jnp.int32), vm((T, T), jnp.int32),
            vm((T, 2 * HEAD_DIM), F32), vm((D,), F32), vm((D,), F32),
            vm((QC, D), BF16),
            vm((D, FC), BF16), vm((D, FC), BF16), vm((FC, D), BF16),
            vm((T, D), BF16), vm((QC // HEAD_DIM, T, HEAD_DIM), BF16), vm((4, T, 2 * KC), BF16), vm((T, 4 * T), F32), vm((T, QC), BF16),
            vm((T, D), F32), vm((2, H, D), F32), vm((H, D), F32), vm((T, D), BF16), vm((T, FC), BF16),
            vm((T, D), BF16),
            dma((13,)), dma((2,)), dma((4,)), dma((1,)), dma((3,)), dma((4,)),
            dma((2, NP1)), dma((2, NP1)), dma((3, NR)), dma((2, NR)),
            dma((2, NP2)), dma((2, NP2)), dma((3, NP2)), dma((2, NP2)),
        ],
        compiler_params=pltpu.CompilerParams(collective_id=0, has_side_effects=True, vmem_limit_bytes=54500000),
    )(*[pltpu.with_memory_space_constraint(a, pltpu.HBM) for a in operands])
    return y, k.reshape(4 * T, 1, HEAD_DIM), v.reshape(4 * T, 1, HEAD_DIM)


def solution(mesh):
    row_spec = P(("rep", "sp"), None)
    tok_spec = P(("rep", "sp"))
    col_spec = P(None, "tp")
    wrow_spec = P("tp", None)
    cache_spec = P("rep", ("tp", "sp"), None)
    return jax.shard_map(local_layer, mesh=mesh,
                         in_specs=(row_spec, tok_spec, tok_spec, P(None), col_spec, col_spec, col_spec, wrow_spec,
                                   P(None), col_spec, col_spec, wrow_spec),
                         out_specs=(row_spec, cache_spec, cache_spec), check_vma=False)
```

time: 108 us -> 87 us (0.81)
  Pallas kernels: 94.7 us -> 84.1 us
  local copies, waits for them, and re-layouts: 10.3 us -> 2.15 us
  other arithmetic: 1.75 us -> 0 us
    pallas_call x1, Pallas kernels: 94.7 us -> 84.1 us  [local_layer(): pl.pallas_call(kernel, out_shape=[jax.ShapeDtypeStruct((T, D), BF16), jax...]
    unnamed x3, local copies, waits for them, and re-layouts: 5.1 us -> 2.15 us
    reshape x2 -> x0, local copies, waits for them, and re-layouts: 2.62 us -> none  [the longest x1 1.31 us: local_layer(): gain_attn.reshape(1, D)]
    broadcast_in_dim x2 -> x0, local copies, waits for them, and re-layouts: 2.61 us -> none  [the longest x1 1.37 us: local_layer(): segq = jnp.broadcast_to(segments[:, None], (T, T))]
where the time goes in v2:
time: 87 us; the launch traced here: 86.9 us
  Pallas kernels  84.1 us (97%)
  local copies, waits for them, and re-layouts  2.15 us (2%)
    pallas_call x1, Pallas kernels, local_layer(): pl.pallas_call(kernel, out_shape=[jax.ShapeDtypeStruct((T, D), BF16), jax...  84.1 us
    unnamed x3, local copies, waits for them, and re-layouts  2.15 us

profile of v2, /device:TPU:0, one launch (start us, length us, event | category | flops | bytes accessed | tf_op | source)
XLA Modules:
  0.0 86.9 jit_solution(14630948211505299496)
XLA Ops:
  0.6 84.1 %shard_map.148 = (bf16[128,2560]{1,0:T(8,128)(2,1)S(1)}, bf16[512,128]{1,0:T(8,128)(2,1)S(1)}, bf16[512,128]{1,0:T(8,128)(2,1)S(1)}) custom-call(bf16[128,2560]{1,0:T(8,128)(2,1)} %x_hbm.1, s32[128]{0:T(128)} %pos_hbm.1, f32[1,128]{1,0:T(1,128)} %constant.2.clone.freq_hbm, s32[128]{0:T(128)} %seg_hbm.1, f32[2560]{0:T(1024)} %ga_hbm.1, ...), custom_call_target="tpu_custom_call" | custom-call | tf_op jit(solution)/shard_map/pallas_call | solution.py:337
  84.7 0.8 copy.19
  85.6 0.7 copy.20
  86.2 0.7 copy.21
